TPU v7x, 32 devices: a whole 2x2x4 slice. The times are simulated.
32 devices in a mesh: wave: 16 (over z, x, core), lev: 2 (over y).
Axes of the slice: x: 2, y: 2, z: 4, core: 2. Of those that a mesh axis runs over, the one named last changes fastest.
Arguments:
- spectral: float32 [136, 256, 2562], P('lev', 'wave'), may hold values from -6 to 6
- to_modes: float32 [136, 136], replicated, may hold values from -3 to 3
- from_modes: float32 [136, 136], replicated, may hold values from -3 to 3
- depth: float32 [136], replicated, may hold values from 0.02 to 50
- owner: int32 [128], replicated, may hold values from 0 to 15, as said below
Outputs:
- solved: float32 [136, 128, 2562], P('lev', 'wave')
Inputs may be any that keep to these rules, and one draw needn't show every extreme that they name: `owner`: group q holds the pairs q * 1 to q * 1 + 1 - 1; a device stores its groups in increasing q from its first slot on, 1 slots each, and leaves its other slots unused. The 8 groups with the same q // 8 have 8 different owners. A device owns at most 16 groups, and some device exactly that many.
All inputs are finite; a program needn't handle non-finite values.
Results may differ from a plain program's by a relative error of at most 0.000075.
Values sent between devices are 32-bit elements; how exact they have to be, the bound alone decides.
A program may use at most 128 MiB of HBM per device.

v0:
```python
import jax
import jax.numpy as jnp
from jax import lax
from jax.sharding import PartitionSpec as P

NT = 1279
KPAIR = 1


def degree_ratio(pairs_here, columns, width):
    slot_index = columns // width
    within = columns % width % (NT + 2)
    match = slot_index[None, :] == jnp.arange(pairs_here.shape[0], dtype=jnp.int32)[:, None]
    pair = jnp.sum(jnp.where(match, pairs_here[:, None], 0), axis=0)
    degree = jnp.where(within <= NT - pair, pair + within, within - 1)
    return (degree * (degree + 1)).astype(jnp.float32) / float(NT * (NT + 1))


def per_device(spectral, to_modes, from_modes, depth, owner):
    waves = lax.axis_size("wave")
    groups = waves // 2
    own_index = lax.axis_index("wave")
    numbers = jnp.arange(groups * waves, dtype=jnp.int32)
    same = owner[:, None] == owner[None, :]
    rank = jnp.sum((same & (numbers[None, :] < numbers[:, None])).astype(jnp.int32), axis=1)
    mine = owner == own_index
    pairs_target = own_index * groups * KPAIR + jnp.arange(groups * KPAIR, dtype=jnp.int32)
    offsets = jnp.arange(KPAIR, dtype=jnp.int32)
    mine_grid = mine.reshape(waves, groups)
    rank_grid = rank.reshape(waves, groups)
    first_slot = jnp.sum(jnp.where(mine_grid, rank_grid, 0), axis=1) * KPAIR
    picks = (first_slot[:, None] + offsets[None, :]).reshape(waves * KPAIR)
    outgoing = jnp.take(spectral, picks, axis=1)
    incoming = lax.all_to_all(outgoing, "wave", split_axis=1, concat_axis=1, tiled=True)
    senders = lax.dynamic_slice_in_dim(owner, own_index * groups, groups)
    places = (senders[:, None] * KPAIR + offsets[None, :]).reshape(groups * KPAIR)
    balanced = jnp.take(incoming, places, axis=1)
    level_rows, number, width = balanced.shape
    flat = balanced.reshape(level_rows, number * width)
    lev_index = lax.axis_index("lev")
    columns = lax.all_to_all(flat, "lev", split_axis=1, concat_axis=0, tiled=True)
    share = columns.shape[1]
    placed = lev_index * share + jnp.arange(share, dtype=jnp.int32)
    ratio = degree_ratio(pairs_target, placed, width)
    modes = jnp.dot(
        to_modes, columns, precision=lax.Precision.HIGHEST, preferred_element_type=jnp.float32
    )
    scaled = modes / (1.0 + depth[:, None] * ratio[None, :])
    mixed = jnp.dot(
        from_modes, scaled, precision=lax.Precision.HIGHEST, preferred_element_type=jnp.float32
    )
    result = lax.all_to_all(mixed, "lev", split_axis=0, concat_axis=1, tiled=True)
    return result.reshape(level_rows, number, width)


def solution(mesh):
    placed = (P("lev", "wave", None), P(), P(), P(), P())
    return jax.shard_map(
        per_device, mesh=mesh, in_specs=placed, out_specs=P("lev", "wave", None), check_vma=False
    )
```

profile of v0, /device:TPU:10, one launch (start us, length us, event | category | flops | bytes accessed | tf_op | source)
XLA Modules:
  0.0 533.1 jit_solution(551096521813116234)
XLA Ops:
  0.0 0.0 copy-start
  0.0 0.9 convert_reduce_fusion
  0.9 0.7 compare_select_fusion.3
  1.6 0.1 select_n.83
  1.7 0.1 reduce_sum.30
  1.8 17.4 %gather_fusion = f32[16,68,2562]{2,0,1:T(8,128)} fusion(f32[68,16,2562]{2,1,0:T(8,128)} %param.5, s32[1024]{0:T(1024)S(1)} %pad_clamp_fusion.1), kind=kCustom, calls=%fused_computation | custom fusion | bytes 22299712 | tf_op jit(solution)/shard_map/jit(_take)/gather | solution.py:33
  19.2 9.5 %select_bitcast_fusion = f32[68,16,2562]{2,1,0:T(8,128)} fusion(f32[16,68,2562]{2,0,1:T(8,128)} %gather_fusion, pred[16]{0:T(512)(128)(4,1)S(1)} %compare_and_fusion), kind=kLoop, calls=%fused_computation.5 | loop fusion | flops 2787456 | bytes 22299664 | tf_op jit(solution)/shard_map/jit(_take)/select_n | solution.py:33
  28.7 12.7 %copy.16 = f32[68,16,2562]{2,0,1:T(8,128)} copy(f32[68,16,2562]{2,1,0:T(8,128)} %select_bitcast_fusion) | data formatting | bytes 22299648 | tf_op jit(solution)/shard_map/jit(_take)/select_n | solution.py:33
  41.4 7.9 %all-to-all-start = ((f32[68,16,2562]{2,0,1:T(8,128)}), f32[68,16,2562]{2,0,1:T(8,128)}, u32[]{:S(2)}, u32[]{:S(2)}) async-start(f32[68,16,2562]{2,0,1:T(8,128)} %copy.16), calls=%async_computation | async-start | bytes 24772608 | tf_op jit(solution)/shard_map/all_to_all | solution.py:34
  49.3 0.0 copy-done.2
  49.3 0.1 compare_and_fusion.1
  49.4 0.1 broadcast_in_dim.53
  49.4 0.1 broadcast_in_dim.54
  49.5 0.2 broadcast_in_dim.55
  49.7 267.3 %all-to-all-done = f32[68,16,2562]{2,0,1:T(8,128)} async-done(((f32[68,16,2562]{2,0,1:T(8,128)}), f32[68,16,2562]{2,0,1:T(8,128)}, u32[]{:S(2)}, u32[]{:S(2)}) %all-to-all-start) | async-done | bytes 11149856 | tf_op jit(solution)/shard_map/all_to_all | solution.py:34
  317.0 8.1 %gather_fusion.1 = f32[8,68,2562]{2,1,0:T(8,128)} fusion(f32[68,16,2562]{2,0,1:T(8,128)} %all-to-all-done, s32[1024]{0:T(1024)S(1)} %pad_clamp_fusion), kind=kCustom, calls=%fused_computation.1 | custom fusion | bytes 11149856 | tf_op jit(solution)/shard_map/jit(_take)/gather | solution.py:37
  325.1 6.4 %copy.17 = f32[68,8,2562]{2,1,0:T(8,128)} copy(f32[68,8,2562]{2,0,1:T(8,128)} %bitcast.20) | data formatting | bytes 11149824 | tf_op jit(solution)/shard_map/jit(_take)/gather | solution.py:37
  331.5 8.8 %gather.12 = f32[68,2,10248]{2,1,0:T(2,128)} reshape(f32[68,8,2562]{2,1,0:T(8,128)} %copy.17) | data formatting | bytes 11149824 | tf_op jit(solution)/shard_map/jit(_take)/gather | solution.py:37
  340.3 5.1 broadcast_select_fusion
  345.4 3.0 copy.18
  348.3 6.4 %all-to-all-start.1 = ((f32[68,2,10248]{2,0,1:T(8,128)}), f32[68,2,10248]{2,0,1:T(8,128)}, u32[]{:S(2)}, u32[]{:S(2)}) async-start(f32[68,2,10248]{2,0,1:T(8,128)} %copy.18), calls=%async_computation.1 | async-start | bytes 11943936 | tf_op jit(solution)/shard_map/all_to_all | solution.py:41
  354.8 0.2 select_reduce_fusion
  355.0 0.1 fusion.4
  355.1 66.8 %all-to-all-done.1 = f32[68,2,10248]{2,0,1:T(8,128)} async-done(((f32[68,2,10248]{2,0,1:T(8,128)}), f32[68,2,10248]{2,0,1:T(8,128)}, u32[]{:S(2)}, u32[]{:S(2)}) %all-to-all-start.1) | async-done | bytes 5574944 | tf_op jit(solution)/shard_map/all_to_all | solution.py:41
  421.9 5.8 %all_to_all.30 = f32[136,10248]{1,0:T(8,128)} reshape(f32[2,68,10248]{2,1,0:T(8,128)} %bitcast.4) | data formatting | bytes 11149824 | tf_op jit(solution)/shard_map/all_to_all | solution.py:41
  427.6 0.0 copy-done.3
  427.6 8.1 %fusion = f32[136,10248]{1,0:T(8,128)S(1)} fusion(f32[136,10248]{1,0:T(8,128)} %all_to_all.30, f32[136,136]{1,0:T(8,128)S(1)} %copy-done, f32[10248]{0:T(1024)S(1)} %fusion.4, f32[136]{0:T(256)S(1)} %copy-done.3), kind=kOutput, calls=%fused_computation.4 | convolution fusion | flops 2278745344 | bytes 11265344 | tf_op jit(solution)/shard_map/dot_general | solution.py:45
  435.7 7.1 %convolution_bitcast_fusion = f32[136,10248]{1,0:T(8,128)} fusion(f32[136,10248]{1,0:T(8,128)S(1)} %fusion, f32[136,136]{1,0:T(8,128)S(1)} %copy-done.1), kind=kOutput, calls=%fused_computation.2 | convolution fusion | flops 2274564096 | bytes 11223808 | tf_op jit(solution)/shard_map/dot_general | solution.py:49
  442.9 5.7 %all_to_all.31 = f32[2,68,10248]{2,1,0:T(8,128)} reshape(f32[136,10248]{1,0:T(8,128)} %convolution_bitcast_fusion) | data formatting | bytes 11149824 | tf_op jit(solution)/shard_map/all_to_all | solution.py:52
  448.6 70.7 %all_to_all.37 = f32[2,68,10248]{2,1,0:T(8,128)S(1)} all-to-all(f32[2,68,10248]{2,1,0:T(8,128)} %all_to_all.31), channel_id=1, replica_groups=mesh['wave'=16,'lev'=2] {'lev'}, dimensions={0} | all-to-all | bytes 11149824 | tf_op jit(solution)/shard_map/all_to_all | solution.py:52
  519.3 5.4 %copy.19 = f32[68,2,10248]{2,1,0:T(2,128)} copy(f32[68,2,10248]{2,0,1:T(8,128)S(1)} %bitcast.19) | data formatting | bytes 11149824 | tf_op jit(solution)/shard_map/all_to_all | solution.py:52
  524.7 8.4 %reshape.90 = f32[68,8,2562]{2,1,0:T(8,128)} reshape(f32[68,2,10248]{2,1,0:T(2,128)} %copy.19) | data formatting | bytes 11149824 | tf_op jit(solution)/shard_map/reshape | solution.py:53
  (11 shorter events, 0.1 us)
Async XLA Ops:
  0.0 427.6 %copy-start = (f32[136,136]{1,0:T(8,128)S(1)}, f32[136,136]{1,0:T(8,128)}, u32[]{:S(2)}) copy-start(f32[136,136]{1,0:T(8,128)} %param.6) | copy-start | bytes 221956
  41.4 7.9 %copy-start.2 = (s32[128]{0:T(128)S(1)}, s32[128]{0:T(128)}, u32[]{:S(2)}) copy-start(s32[128]{0:T(128)} %param.9) | copy-start | bytes 1540
  41.4 275.6 %all-to-all-start = ((f32[68,16,2562]{2,0,1:T(8,128)}), f32[68,16,2562]{2,0,1:T(8,128)}, u32[]{:S(2)}, u32[]{:S(2)}) async-start(f32[68,16,2562]{2,0,1:T(8,128)} %copy.16), calls=%async_computation | async-start | bytes 24772608 | tf_op jit(solution)/shard_map/all_to_all | solution.py:34
  348.3 73.5 %all-to-all-start.1 = ((f32[68,2,10248]{2,0,1:T(8,128)}), f32[68,2,10248]{2,0,1:T(8,128)}, u32[]{:S(2)}, u32[]{:S(2)}) async-start(f32[68,2,10248]{2,0,1:T(8,128)} %copy.18), calls=%async_computation.1 | async-start | bytes 11943936 | tf_op jit(solution)/shard_map/all_to_all | solution.py:41
  421.8 5.8 %copy-start.3 = (f32[136]{0:T(256)S(1)}, f32[136]{0:T(256)}, u32[]{:S(2)}) copy-start(f32[136]{0:T(256)} %param.8) | copy-start | bytes 1636
  427.6 8.1 %copy-start.1 = (f32[136,136]{1,0:T(8,128)S(1)}, f32[136,136]{1,0:T(8,128)}, u32[]{:S(2)}) copy-start(f32[136,136]{1,0:T(8,128)} %param.7) | copy-start | bytes 221956
where the time goes:
time: 534 us; the launch traced here: 533 us
  waiting for transfers between devices  334 us (63%)
  local copies, waits for them, and re-layouts  82 us (15%)
  blocking collectives  70.7 us (13%)
  other arithmetic  16.7 us (3%)
  matrix products  15.2 us (3%)
  starting transfers between devices  14.3 us (3%)
    all_to_all x1, waiting for transfers between devices, per_device(): lax.all_to_all(outgoing, 'wave', split_axis=1, concat_axis=1, tiled=True)  267 us
    all_to_all x1, blocking collectives, per_device(): lax.all_to_all(mixed, 'lev', split_axis=0, concat_axis=1, tiled=True)  70.7 us
    all_to_all x1, waiting for transfers between devices, per_device(): lax.all_to_all(flat, 'lev', split_axis=1, concat_axis=0, tiled=True)  66.8 us
    gather x3, local copies, waits for them, and re-layouts, per_device(): balanced = jnp.take(incoming, places, axis=1)  23.3 us
    gather x1, local copies, waits for them, and re-layouts, per_device(): outgoing = jnp.take(spectral, picks, axis=1)  17.4 us
    select_n x1, local copies, waits for them, and re-layouts, per_device(): outgoing = jnp.take(spectral, picks, axis=1)  12.7 us
    all_to_all x2, local copies, waits for them, and re-layouts, per_device(): lax.all_to_all(mixed, 'lev', split_axis=0, concat_axis=1, tiled=True)  11.1 us
  transfers between devices with their start and end apart: 2, of which 2 were waited for; matrix products, arithmetic and copies ran while one was open for 0% of the time, Pallas kernels for 0%

commit v1 on v0

v1 whole, which is shorter than its diff:
```python
import functools

import jax
import jax.numpy as jnp
from jax import lax
from jax.experimental import pallas as pl
from jax.experimental.pallas import tpu as pltpu
from jax.sharding import PartitionSpec as P

NT = 1279
KPAIR = 1
LANES = 128
TILES = 3
AHEAD = 2
MESH = pl.DeviceIdType.MESH


def flipped(index, mask, count):
    result = index * 0
    bit = 1
    while bit < count:
        own = lax.rem(lax.div(index, bit), 2)
        result = result + bit * ((1 - own) if mask & bit else own)
        bit *= 2
    return result


def halves(value):
    high = value.astype(jnp.bfloat16)
    low = (value - high.astype(jnp.float32)).astype(jnp.bfloat16)
    return high, low


def product(left_both, left_high, right, rows):
    high, low = halves(right)
    both = jnp.dot(left_both, high, preferred_element_type=jnp.float32)
    cross = jnp.dot(left_high, low, preferred_element_type=jnp.float32)
    return (both[rows:] + cross) + both[:rows]


def kernel(sizes, picks, places, spectral, last, to_modes, from_modes, depth, solved, *scratch):
    waves, levs, pairs, slots, levels, width, chunk, chunks = sizes
    received, rows_in = scratch[:chunks], scratch[chunks : 2 * chunks]
    sending, mine, theirs, to_both, from_both, staged = scratch[2 * chunks : 2 * chunks + 6]
    load_sem, send_sem, recv_sem, lev_send, lev_recv, out_sem = scratch[2 * chunks + 6 :]
    me = lax.axis_index("wave")
    lev = lax.axis_index("lev")
    modes_number = depth.shape[0]

    tiles = chunk // LANES

    def load(tile):
        whole = (tile + 1) * LANES <= width
        source = spectral.at[:, pl.ds(tile * LANES, LANES)] if whole else last
        return pltpu.make_async_copy(source, rows_in[tile // tiles].at[tile % tiles], load_sem.at[tile])

    for tile in range(chunks * tiles):
        load(tile).start()

    barrier = pltpu.get_barrier_semaphore()
    for mask in range(1, waves):
        pl.semaphore_signal(
            barrier, inc=1, device_id={"wave": flipped(me, mask, waves)}, device_id_type=MESH
        )
    for turn in range(1, levs):
        pl.semaphore_signal(
            barrier, inc=1, device_id={"lev": lax.rem(lev + turn, levs)}, device_id_type=MESH
        )

    for part in range(levs):
        high, low = halves(to_modes[part])
        to_both[part, :modes_number] = high
        to_both[part, modes_number:] = low
    high, low = halves(from_modes[...])
    from_both[0], from_both[1] = high, low
    pl.semaphore_wait(barrier, waves + levs - 2)

    def send(c):
        def pick(mask, target):
            slot = picks[flipped(me, mask, waves)]
            for tile in range(tiles):
                target[:, pl.ds(tile * LANES, LANES)] = rows_in[c][
                    tile, pl.ds(slot, levels, stride=slots), :
                ]

        for tile in range(c * tiles, (c + 1) * tiles):
            load(tile).wait()
        for mask in range(waves - 1, 0, -1):
            pick(mask, sending.at[c, mask - 1])
            pltpu.make_async_remote_copy(
                src_ref=sending.at[c, mask - 1],
                dst_ref=received[c].at[mask],
                send_sem=send_sem.at[c],
                recv_sem=recv_sem.at[c],
                device_id={"wave": flipped(me, mask, waves)},
                device_id_type=MESH,
            ).start()
        pick(0, received[c].at[0])

    def lev_copy(c, turn):
        return pltpu.make_async_remote_copy(
            src_ref=mine.at[c],
            dst_ref=theirs.at[c, turn - 1],
            send_sem=lev_send.at[c, turn - 1],
            recv_sem=lev_recv.at[c, turn - 1],
            device_id={"lev": lax.rem(lev + turn, levs)},
            device_id_type=MESH,
        )

    def out_copy(c):
        return pltpu.make_async_copy(
            staged.at[c], solved.at[:, :, pl.ds(c * chunk, chunk)], out_sem.at[c]
        )

    def gather(c):
        arrived = received[c].at[pl.ds(1, waves - 1)]
        pltpu.make_async_copy(arrived, arrived, recv_sem.at[c]).wait()

        @pl.loop(0, pairs)
        def _(pair):
            mine[c, pair] = received[c][places[pair]]

        for turn in range(1, levs):
            lev_copy(c, turn).start()

    def solve(c):
        for turn in range(1, levs):
            lev_copy(c, turn).wait_recv()
        column = lax.broadcasted_iota(jnp.int32, (1, chunk), 1) + c * chunk
        within = jnp.where(column >= NT + 2, column - (NT + 2), column)

        @pl.loop(0, pairs)
        def _(pair):
            wavenumber = me * pairs + pair
            degree = jnp.where(within <= NT - wavenumber, wavenumber + within, within - 1)
            ratio = (degree * (degree + 1)).astype(jnp.float32) / float(NT * (NT + 1))
            modes = None
            for turn in range(levs):
                source = lax.rem(lev + levs - turn, levs)
                block = mine[c, pair] if turn == 0 else theirs[c, turn - 1, pair]
                matrix = to_both.at[source]
                term = product(matrix[...], matrix[:modes_number], block, modes_number)
                modes = term if modes is None else modes + term
            scaled = modes / (1.0 + depth[...] * ratio)
            high, low = halves(scaled)
            from_high = from_both[0]
            result = jnp.dot(from_both[1], high, preferred_element_type=jnp.float32)
            result += jnp.dot(from_high, low, preferred_element_type=jnp.float32)
            result += jnp.dot(from_high, high, preferred_element_type=jnp.float32)
            staged[c, pair] = result

        out_copy(c).start()

    for c in range(min(AHEAD, chunks)):
        send(c)
    for c in range(chunks):
        if c + AHEAD < chunks:
            send(c + AHEAD)
        gather(c)
        if c >= 1:
            solve(c - 1)
    solve(chunks - 1)
    for c in range(chunks):
        pltpu.make_async_copy(sending.at[c], sending.at[c], send_sem.at[c]).wait()
        for turn in range(1, levs):
            lev_copy(c, turn).wait_send()
        out_copy(c).wait()


def per_device(spectral, to_modes, from_modes, depth, owner):
    waves, levs = lax.axis_size("wave"), lax.axis_size("lev")
    levels, slots, width = spectral.shape
    groups = owner.shape[0] // waves
    pairs = groups * KPAIR
    modes_number = depth.shape[0]
    own_index, lev_index = lax.axis_index("wave"), lax.axis_index("lev")
    numbers = jnp.arange(owner.shape[0], dtype=jnp.int32)
    mine = owner == own_index
    before = (numbers[:, None] > numbers[None, :]) & mine[None, :]
    rank = jnp.sum(before.astype(jnp.int32), axis=1)
    picks = jnp.sum(jnp.where(mine, rank, 0).reshape(waves, groups), axis=1)
    places = lax.dynamic_slice_in_dim(owner, own_index * groups, groups) ^ own_index
    chunk = TILES * LANES
    chunks = pl.cdiv(width, chunk)
    sizes = (waves, levs, pairs, slots, levels, width, chunk, chunks)
    rows = spectral.reshape(levels * slots, width)
    full = width // LANES * LANES
    last = jnp.pad(rows[:, full:], ((0, 0), (0, full + LANES - width)))
    by_lev = to_modes.reshape(modes_number, levs, levels).transpose(1, 0, 2)
    own_rows = lax.dynamic_slice_in_dim(from_modes, lev_index * levels, levels)
    vmem, smem, anywhere = (
        pl.BlockSpec(memory_space=space) for space in (pltpu.VMEM, pltpu.SMEM, pl.ANY)
    )
    dma = pltpu.SemaphoreType.DMA
    f32, bf16 = jnp.float32, jnp.bfloat16
    solved = pl.pallas_call(
        functools.partial(kernel, sizes),
        out_shape=jax.ShapeDtypeStruct((pairs, levels, chunks * chunk), f32),
        in_specs=[smem, smem, anywhere, anywhere, vmem, vmem, vmem],
        out_specs=anywhere,
        scratch_shapes=[pltpu.VMEM((waves, levels, chunk), f32) for _ in range(chunks)]
        + [pltpu.VMEM((TILES, levels * slots, LANES), f32) for _ in range(chunks)]
        + [
            pltpu.VMEM((chunks, waves - 1, levels, chunk), f32),
            pltpu.VMEM((chunks, pairs, levels, chunk), f32),
            pltpu.VMEM((chunks, levs - 1, pairs, levels, chunk), f32),
            pltpu.VMEM((levs, 2 * modes_number, levels), bf16),
            pltpu.VMEM((2, levels, modes_number), bf16),
            pltpu.VMEM((chunks, pairs, levels, chunk), f32),
            dma((chunks * TILES,)),
            dma((chunks,)),
            dma((chunks,)),
            dma((chunks, levs - 1)),
            dma((chunks, levs - 1)),
            dma((chunks,)),
        ],
        compiler_params=pltpu.CompilerParams(
            collective_id=0, has_side_effects=True, vmem_limit_bytes=67043328
        ),
    )(picks, places, rows, last, by_lev, own_rows, depth[:, None])
    return solved[:, :, :width].transpose(1, 0, 2)


def solution(mesh):
    placed = (P("lev", "wave", None), P(), P(), P(), P())
    return jax.shard_map(
        per_device, mesh=mesh, in_specs=placed, out_specs=P("lev", "wave", None), check_vma=False
    )
```

time: 534 us -> 324 us (0.61)
  the two profiles are of different devices: /device:TPU:10 before, /device:TPU:0 now
where the time goes in v1:
time: 324 us
  Pallas kernels  307 us (95%)
  local copies, waits for them, and re-layouts  13.4 us (4%)
  other arithmetic  3.46 us (1%)
    pallas_call x1, Pallas kernels, per_device(): pl.pallas_call(functools.partial(kernel, sizes), out_shape=jax.ShapeDtype...  307 us
    transpose x2, local copies, waits for them, and re-layouts, per_device(): return solved[:, :, :width].transpose(1, 0, 2)  6.77 us

profile of v1, /device:TPU:0, one launch (start us, length us, event | category | flops | bytes accessed | tf_op | source)
XLA Modules:
  0.0 324.0 jit_solution(3978282844490800034)
XLA Ops:
  0.0 1.3 dynamic-slice_xor_fusion.places
  1.3 0.7 broadcast_compare_fusion
  2.0 0.1 convert_reduce_fusion
  2.1 0.7 broadcast_select_fusion
  2.8 0.1 reshape.10
  2.8 0.7 reduce_sum.19.picks
  3.5 1.4 copy.13.depth
  5.0 1.5 constant_dynamic-slice_fusion.from_modes
  6.5 1.0 reshape.13
  7.5 0.7 copy.18
  8.2 1.1 slice.8
  9.3 0.8 pad.4.last
  10.1 307.1 %shard_map.55 = f32[8,68,2688]{2,1,0:T(8,128)} custom-call(s32[16]{0:T(128)} %reduce_sum.19.picks, s32[8]{0:T(128)} %dynamic-slice_xor_fusion.places, f32[1088,2562]{1,0:T(8,128)} %bitcast.8, f32[1088,128]{1,0:T(8,128)} %pad.4.last, f32[2,136,68]{2,1,0:T(8,128)} %bitcast.9, f32[68,136]{1,0:T(8,128)} %constant_dynamic-slice_fusion.from_modes, ...), custom_call_target="tpu_custom_call" | custom-call | tf_op jit(solution)/shard_map/pallas_call | solution.py:196
  317.2 3.2 slice_bitcast_fusion
  320.4 3.6 %copy.14 = f32[68,8,2562]{2,1,0:T(8,128)} copy(f32[68,8,2562]{2,0,1:T(8,128)S(1)} %slice_bitcast_fusion) | data formatting | bytes 11149824 | tf_op jit(solution)/shard_map/transpose | solution.py:221

commit v2 on v1

v2 whole, which is shorter than its diff:
```python
import functools

import jax
import jax.numpy as jnp
from jax import lax
from jax.experimental import pallas as pl
from jax.experimental.pallas import tpu as pltpu
from jax.sharding import PartitionSpec as P

NT = 1279
KPAIR = 1
LANES = 128
TILES = 3
AHEAD = 2
MESH = pl.DeviceIdType.MESH


def flipped(index, mask, count):
    result = index * 0
    bit = 1
    while bit < count:
        own = lax.rem(lax.div(index, bit), 2)
        result = result + bit * ((1 - own) if mask & bit else own)
        bit *= 2
    return result


def halves(value):
    high = value.astype(jnp.bfloat16)
    low = (value - high.astype(jnp.float32)).astype(jnp.bfloat16)
    return high, low


def product(left_both, left_high, right, rows):
    high, low = halves(right)
    both = jnp.dot(left_both, high, preferred_element_type=jnp.float32)
    cross = jnp.dot(left_high, low, preferred_element_type=jnp.float32)
    return (both[rows:] + cross) + both[:rows]


def kernel(sizes, picks, places, spectral, last, to_modes, from_modes, depth, solved, *scratch):
    waves, levs, pairs, slots, levels, width, parts, packs, rest = sizes
    chunks = len(parts)
    received, rows_in, sending, mine, theirs, staged = (
        scratch[kind * chunks : (kind + 1) * chunks] for kind in range(6)
    )
    rows_last, tail_sent, tail_got, tail_mine, tail_theirs = scratch[6 * chunks : 6 * chunks + 5]
    to_both, from_both, load_sem, send_sem, recv_sem, lev_send, lev_recv, out_sem = scratch[
        6 * chunks + 5 :
    ]
    me = lax.axis_index("wave")
    lev = lax.axis_index("lev")
    modes_number = depth.shape[0]
    firsts = [sum(parts[:c]) for c in range(chunks)]
    final = chunks - 1

    def load(c, tile):
        number = firsts[c] + tile
        if number < sum(parts):
            source = spectral.at[:, pl.ds(number * LANES, LANES)]
            return pltpu.make_async_copy(source, rows_in[c].at[tile], load_sem.at[number])
        target = rows_last.at[pl.ds(0, levels * slots)]
        return pltpu.make_async_copy(last, target, load_sem.at[number])

    def width_of(c):
        return parts[c] + (1 if c == final else 0)

    for c in range(chunks):
        for tile in range(width_of(c)):
            load(c, tile).start()

    barrier = pltpu.get_barrier_semaphore()
    for mask in range(1, waves):
        pl.semaphore_signal(
            barrier, inc=1, device_id={"wave": flipped(me, mask, waves)}, device_id_type=MESH
        )
    for turn in range(1, levs):
        pl.semaphore_signal(
            barrier, inc=1, device_id={"lev": lax.rem(lev + turn, levs)}, device_id_type=MESH
        )

    for part in range(levs):
        high, low = halves(to_modes[part])
        to_both[part, :modes_number] = high
        to_both[part, modes_number:] = low
    high, low = halves(from_modes[...])
    from_both[0], from_both[1] = high, low
    pl.semaphore_wait(barrier, waves + levs - 2)

    def packed(slot):
        lane = lax.broadcasted_iota(jnp.int32, (8, LANES), 1)
        total = rows_last[pl.ds(slot, 8, stride=slots), :]
        for k in range(1, packs):
            block = rows_last[pl.ds(8 * k * slots + slot, 8, stride=slots), :]
            total = jnp.where(lane >= k * rest, pltpu.roll(block, k * rest, 1), total)
        return total

    def unpacked(block):
        pieces = [block] + [pltpu.roll(block, LANES - k * rest, 1) for k in range(1, packs)]
        return jnp.concatenate(pieces, axis=0)[:levels]

    def send(c):
        for tile in range(width_of(c)):
            load(c, tile).wait()

        def pick(mask, target):
            slot = picks[flipped(me, mask, waves)]
            for tile in range(parts[c]):
                target[:, pl.ds(tile * LANES, LANES)] = rows_in[c][
                    tile, pl.ds(slot, levels, stride=slots), :
                ]

        def push(mask, source, target, number):
            pltpu.make_async_remote_copy(
                src_ref=source.at[mask - 1],
                dst_ref=target.at[mask],
                send_sem=send_sem.at[number],
                recv_sem=recv_sem.at[number],
                device_id={"wave": flipped(me, mask, waves)},
                device_id_type=MESH,
            ).start()

        if c == final:
            for mask in range(waves - 1, 0, -1):
                tail_sent[mask - 1] = packed(picks[flipped(me, mask, waves)])
                push(mask, tail_sent, tail_got, chunks)
            tail_got[0] = packed(picks[me])
        for mask in range(waves - 1, 0, -1):
            pick(mask, sending[c].at[mask - 1])
            push(mask, sending[c], received[c], c)
        pick(0, received[c].at[0])

    def lev_copy(c, turn):
        source, target = (tail_mine, tail_theirs) if c == chunks else (mine[c], theirs[c])
        return pltpu.make_async_remote_copy(
            src_ref=source,
            dst_ref=target.at[turn - 1],
            send_sem=lev_send.at[c, turn - 1],
            recv_sem=lev_recv.at[c, turn - 1],
            device_id={"lev": lax.rem(lev + turn, levs)},
            device_id_type=MESH,
        )

    def out_copy(c, tile):
        number = firsts[c] + tile
        columns = solved.at[:, pl.ds(number * LANES, LANES)]
        return pltpu.make_async_copy(staged[c].at[tile], columns, out_sem.at[number])

    def gather(c):
        if c == final:
            arrived = tail_got.at[pl.ds(1, waves - 1)]
            pltpu.make_async_copy(arrived, arrived, recv_sem.at[chunks]).wait()
            for pair in range(pairs):
                tail_mine[pair] = tail_got[places[pair]]
            for turn in range(1, levs):
                lev_copy(chunks, turn).start()
        arrived = received[c].at[pl.ds(1, waves - 1)]
        pltpu.make_async_copy(arrived, arrived, recv_sem.at[c]).wait()

        @pl.loop(0, pairs)
        def _(pair):
            mine[c][pair] = received[c][places[pair]]

        for turn in range(1, levs):
            lev_copy(c, turn).start()

    def solve(c):
        for turn in range(1, levs):
            lev_copy(c, turn).wait_recv()
            if c == final:
                lev_copy(chunks, turn).wait_recv()
        size = width_of(c) * LANES
        column = lax.broadcasted_iota(jnp.int32, (1, size), 1) + firsts[c] * LANES
        within = jnp.where(column >= width // 2, column - width // 2, column)

        @pl.loop(0, pairs)
        def _(pair):
            wavenumber = me * pairs + pair
            degree = jnp.where(within <= NT - wavenumber, wavenumber + within, within - 1)
            ratio = (degree * (degree + 1)).astype(jnp.float32) / float(NT * (NT + 1))
            modes = None
            for turn in range(levs):
                source = lax.rem(lev + levs - turn, levs)
                block = mine[c][pair] if turn == 0 else theirs[c][turn - 1, pair]
                if c == final:
                    tail = tail_mine[pair] if turn == 0 else tail_theirs[turn - 1, pair]
                    block = jnp.concatenate([block, unpacked(tail)], axis=1)
                matrix = to_both.at[source]
                term = product(matrix[...], matrix[:modes_number], block, modes_number)
                modes = term if modes is None else modes + term
            scaled = modes / (1.0 + depth[...] * ratio)
            high, low = halves(scaled)
            from_high = from_both[0]
            result = jnp.dot(from_both[1], high, preferred_element_type=jnp.float32)
            result += jnp.dot(from_high, low, preferred_element_type=jnp.float32)
            result += jnp.dot(from_high, high, preferred_element_type=jnp.float32)
            for tile in range(width_of(c)):
                staged[c][tile, pl.ds(pair, levels, stride=pairs), :] = result[
                    :, tile * LANES : (tile + 1) * LANES
                ]

        for tile in range(width_of(c)):
            out_copy(c, tile).start()

    for c in range(min(AHEAD, chunks)):
        send(c)
    for c in range(chunks):
        if c + AHEAD < chunks:
            send(c + AHEAD)
        gather(c)
        if c >= 1:
            solve(c - 1)
    solve(final)
    for c in range(chunks + 1):
        sent = tail_sent if c == chunks else sending[c]
        pltpu.make_async_copy(sent, sent, send_sem.at[c]).wait()
        for turn in range(1, levs):
            lev_copy(c, turn).wait_send()
    for c in range(chunks):
        for tile in range(width_of(c)):
            out_copy(c, tile).wait()


def per_device(spectral, to_modes, from_modes, depth, owner):
    waves, levs = lax.axis_size("wave"), lax.axis_size("lev")
    levels, slots, width = spectral.shape
    groups = owner.shape[0] // waves
    pairs = groups * KPAIR
    modes_number = depth.shape[0]
    own_index, lev_index = lax.axis_index("wave"), lax.axis_index("lev")
    numbers = jnp.arange(owner.shape[0], dtype=jnp.int32)
    mine = owner == own_index
    before = (numbers[:, None] > numbers[None, :]) & mine[None, :]
    rank = jnp.sum(before.astype(jnp.int32), axis=1)
    picks = jnp.sum(jnp.where(mine, rank, 0).reshape(waves, groups), axis=1)
    places = lax.dynamic_slice_in_dim(owner, own_index * groups, groups) ^ own_index
    whole, rest = width // LANES, width % LANES
    packs = pl.cdiv(levels, 8)
    assert 0 < rest and packs * rest <= LANES
    parts = (TILES,) * (whole // TILES) + ((whole % TILES,) if whole % TILES else ())
    chunks = len(parts)
    sizes = (waves, levs, pairs, slots, levels, width, parts, packs, rest)
    rows = spectral.reshape(levels * slots, width)
    last = jnp.pad(rows[:, whole * LANES :], ((0, 0), (0, LANES - rest)))
    by_lev = to_modes.reshape(modes_number, levs, levels).transpose(1, 0, 2)
    own_rows = lax.dynamic_slice_in_dim(from_modes, lev_index * levels, levels)
    vmem, smem, anywhere = (
        pl.BlockSpec(memory_space=space) for space in (pltpu.VMEM, pltpu.SMEM, pl.ANY)
    )
    dma = pltpu.SemaphoreType.DMA
    f32, bf16 = jnp.float32, jnp.bfloat16
    widths = [tiles * LANES for tiles in parts]
    staged_tiles = parts[:-1] + (parts[-1] + 1,)
    solved = pl.pallas_call(
        functools.partial(kernel, sizes),
        out_shape=jax.ShapeDtypeStruct((levels * pairs, (whole + 1) * LANES), f32),
        in_specs=[smem, smem, anywhere, anywhere, vmem, vmem, vmem],
        out_specs=anywhere,
        scratch_shapes=[pltpu.VMEM((waves, levels, size), f32) for size in widths]
        + [pltpu.VMEM((tiles, levels * slots, LANES), f32) for tiles in parts]
        + [pltpu.VMEM((waves - 1, levels, size), f32) for size in widths]
        + [pltpu.VMEM((pairs, levels, size), f32) for size in widths]
        + [pltpu.VMEM((levs - 1, pairs, levels, size), f32) for size in widths]
        + [pltpu.VMEM((tiles, levels * pairs, LANES), f32) for tiles in staged_tiles]
        + [
            pltpu.VMEM((8 * packs * slots, LANES), f32),
            pltpu.VMEM((waves - 1, 8, LANES), f32),
            pltpu.VMEM((waves, 8, LANES), f32),
            pltpu.VMEM((pairs, 8, LANES), f32),
            pltpu.VMEM((levs - 1, pairs, 8, LANES), f32),
            pltpu.VMEM((levs, 2 * modes_number, levels), bf16),
            pltpu.VMEM((2, levels, modes_number), bf16),
            dma((whole + 1,)),
            dma((chunks + 1,)),
            dma((chunks + 1,)),
            dma((chunks + 1, levs - 1)),
            dma((chunks + 1, levs - 1)),
            dma((whole + 1,)),
        ],
        compiler_params=pltpu.CompilerParams(
            collective_id=0, has_side_effects=True, vmem_limit_bytes=67043328
        ),
    )(picks, places, rows, last, by_lev, own_rows, depth[:, None])
    return solved.reshape(levels, pairs, (whole + 1) * LANES)[:, :, :width]


def solution(mesh):
    placed = (P("lev", "wave", None), P(), P(), P(), P())
    return jax.shard_map(
        per_device, mesh=mesh, in_specs=placed, out_specs=P("lev", "wave", None), check_vma=False
    )
```

time: 324 us -> 312 us (0.963)
  Pallas kernels: 307 us -> 296 us
    pallas_call x1, Pallas kernels: 307 us -> 296 us  [per_device(): pl.pallas_call(functools.partial(kernel, sizes), out_shape=jax.ShapeDtype...]
    transpose x2 -> x0, local copies, waits for them, and re-layouts: 6.77 us -> none  [per_device(): return solved[:, :, :width].transpose(1, 0, 2)]
    unnamed x0 -> x1, local copies, waits for them, and re-layouts: none -> 5.59 us
where the time goes in v2:
time: 312 us
  Pallas kernels  296 us (95%)
  local copies, waits for them, and re-layouts  12.3 us (4%)
  other arithmetic  3.32 us (1%)
    pallas_call x1, Pallas kernels, per_device(): pl.pallas_call(functools.partial(kernel, sizes), out_shape=jax.ShapeDtype...  296 us

profile of v2, /device:TPU:0, one launch (start us, length us, event | category | flops | bytes accessed | tf_op | source)
XLA Modules:
  0.0 311.9 jit_solution(14589652580087139613)
XLA Ops:
  0.0 1.3 dynamic-slice_xor_fusion.places
  1.3 0.7 broadcast_compare_fusion
  1.9 0.1 convert_reduce_fusion
  2.0 0.7 broadcast_select_fusion
  2.7 0.1 reshape.13
  2.8 0.6 reduce_sum.19.picks
  3.4 1.4 copy.11.depth
  4.8 1.5 constant_dynamic-slice_fusion.from_modes
  6.4 1.0 reshape.17
  7.4 0.7 copy.15
  8.1 1.1 slice.8
  9.2 0.8 pad.4.last
  10.0 296.3 %shard_map.55 = f32[544,2688]{1,0:T(8,128)} custom-call(s32[16]{0:T(128)} %reduce_sum.19.picks, s32[8]{0:T(128)} %dynamic-slice_xor_fusion.places, f32[1088,2562]{1,0:T(8,128)} %bitcast.9, f32[1088,128]{1,0:T(8,128)} %pad.4.last, f32[2,136,68]{2,1,0:T(8,128)} %bitcast.10, f32[68,136]{1,0:T(8,128)} %constant_dynamic-slice_fusion.from_modes, f32[136,1]{1,0:T(8,128)} %copy.11.depth), custom_call_target="tpu_custom_call" | custom-call | tf_op jit(solution)/shard_map/pallas_call | solution.py:254
  306.3 5.6 %copy.17 = f32[68,8,2562]{2,1,0:T(8,128)} copy(f32[68,8,2562]{2,1,0:T(8,128)} %bitcast.7) | data formatting | bytes 11149824
